TPU v7x, 32 devices: a whole 2x2x4 slice. The times are simulated.
32 devices in a mesh: groups: 2 (over x), req: 8 (over z, y), head: 2 (over core).
Axes of the slice: x: 2, y: 2, z: 4, core: 2. Of those that a mesh axis runs over, the one named last changes fastest.
Arguments:
- queries: bfloat16 [16, 8192], P(('groups', 'req')), parts along dimension 0, may hold values from -120 to 120
- prefix_cache: bfloat16 [16, 4096, 2048], P(('groups', 'req'), 'head'), parts along dimension 0, may hold values from -4.1 to 4.1
- paged_pool_cache: bfloat16 [2, 256, 16, 2048], P('head', ('groups', 'req')), parts along dimension 1, may hold values from -4 to 4
- block_table: int32 [2, 16, 16], P('head', ('groups', 'req')), parts along dimension 1, may hold values from 0 to 15
- lengths: int32 [2, 16], P('head', ('groups', 'req')), parts along dimension 1, may hold values from 1 to 256
- owner: int32 [2], P('groups'), parts along dimension 0, may hold values from 0 to 7
Outputs:
- attended: bfloat16 [16, 8192], P(('groups', 'req')), parts along dimension 0
There are 2 independent parts, one for each index of `groups`. A program takes and returns all parts, laid end to end along the dimension named above; each array names one. Nothing has to cross between parts.
Inputs may be any that keep to these rules, and one draw needn't show every extreme that they name: `block_table`: entries index the pages that the request's own rank holds, as the steps say.
All inputs are finite; a program needn't handle non-finite values.
Results may differ from a plain program's by a relative error of at most 0.014.
Values may be sent and summed in bfloat16 or wider, within the bound.
A program may use at most 64 MiB of HBM per device.

v0:
```python
import math

import jax
import jax.numpy as jnp
from jax import lax
from jax.sharding import PartitionSpec as P

QUERY_HEADS = 64
KEY_VALUE_HEADS = 8
HEAD_SIZE = 128


def spread(block, axis, source):
    block = jnp.where(lax.axis_index(axis) == source, block, jnp.zeros_like(block))
    return lax.psum(block, axis)


def combine(first, second):
    top = jnp.maximum(first[0], second[0])
    early = jnp.exp(first[0] - top)
    later = jnp.exp(second[0] - top)
    total = first[1] * early + second[1] * later
    summed = first[2] * early[..., None] + second[2] * later[..., None]
    return (top, total, summed)


def prefix_parts(block_piece):
    width_total = KEY_VALUE_HEADS * HEAD_SIZE
    key_rows = block_piece[:, :width_total].reshape(
        block_piece.shape[0], KEY_VALUE_HEADS, HEAD_SIZE
    )
    value_rows = block_piece[:, width_total:].reshape(
        block_piece.shape[0], KEY_VALUE_HEADS, HEAD_SIZE
    )
    return (key_rows, value_rows)


def weigh(scores, top):
    return jnp.exp(scores - top[..., None]).astype(jnp.bfloat16)


def prefix_state(page_lookup, block_piece, scale):
    key_rows, value_rows = prefix_parts(block_piece)
    scores = (
        jnp.einsum("rkgd,tkd->rkgt", page_lookup, key_rows, preferred_element_type=jnp.float32)
        * scale
    )
    top = jnp.max(scores, axis=-1)
    weights = weigh(scores, top)
    total = jnp.sum(weights.astype(jnp.float32), axis=-1)
    summed = jnp.einsum("rkgt,tkd->rkgd", weights, value_rows, preferred_element_type=jnp.float32)
    return (top, total, summed)


def body(queries, prefix_cache, paged_pool_cache, block_table, lengths, owner):
    row_count = queries.shape[0]
    width_total = KEY_VALUE_HEADS * HEAD_SIZE
    scale = HEAD_SIZE ** (-0.5)
    page_lookup = queries.reshape(
        row_count, KEY_VALUE_HEADS, QUERY_HEADS // KEY_VALUE_HEADS, HEAD_SIZE
    )
    page_slots = block_table.shape[2] * paged_pool_cache.shape[2]
    gathered_pages = paged_pool_cache[0][block_table[0]].reshape(
        row_count, page_slots, 2 * width_total
    )
    suffix_keys = gathered_pages[:, :, :width_total].reshape(
        row_count, page_slots, KEY_VALUE_HEADS, HEAD_SIZE
    )
    suffix_values = gathered_pages[:, :, width_total:].reshape(
        row_count, page_slots, KEY_VALUE_HEADS, HEAD_SIZE
    )
    position = jnp.arange(page_slots, dtype=jnp.int32)
    live = position[None, :] < lengths[0][:, None]
    suf_scores = (
        jnp.einsum("rkgd,rtkd->rkgt", page_lookup, suffix_keys, preferred_element_type=jnp.float32)
        * scale
    )
    suf_scores = jnp.where(live[:, None, None, :], suf_scores, -jnp.inf)
    root = owner[0]
    local_prefix = prefix_cache[0]
    suf_top = jnp.max(suf_scores, axis=-1)
    suf_w = weigh(suf_scores, suf_top)
    state = (
        suf_top,
        jnp.sum(suf_w.astype(jnp.float32), axis=-1),
        jnp.einsum("rkgt,rtkd->rkgd", suf_w, suffix_values, preferred_element_type=jnp.float32),
    )
    every_query = lax.all_gather(queries, "req", axis=0, tiled=True)
    count = every_query.shape[0]
    block_rows = math.gcd(count, 8)
    grouped = every_query.reshape(
        count // block_rows, block_rows, KEY_VALUE_HEADS, QUERY_HEADS // KEY_VALUE_HEADS, HEAD_SIZE
    )

    def one_block(block_queries):
        return prefix_state(block_queries, local_prefix, scale)

    tops, totals, sums = lax.map(one_block, grouped)
    tops = tops.reshape(count, KEY_VALUE_HEADS, QUERY_HEADS // KEY_VALUE_HEADS)
    totals = totals.reshape(count, KEY_VALUE_HEADS, QUERY_HEADS // KEY_VALUE_HEADS)
    sums = sums.reshape(count, KEY_VALUE_HEADS, QUERY_HEADS // KEY_VALUE_HEADS, HEAD_SIZE)
    tops, totals, sums = (
        spread(tops, "req", root),
        spread(totals, "req", root),
        spread(sums, "req", root),
    )
    start = lax.axis_index("req") * row_count
    mine = (
        lax.dynamic_slice_in_dim(tops, start, row_count, 0),
        lax.dynamic_slice_in_dim(totals, start, row_count, 0),
        lax.dynamic_slice_in_dim(sums, start, row_count, 0),
    )
    state = combine(state, mine)
    highest = lax.pmax(state[0], "head")
    factor = jnp.exp(state[0] - highest)
    total, summed = (
        lax.psum((state[1] * factor).astype(jnp.bfloat16), "head").astype(jnp.float32),
        lax.psum((state[2] * factor[..., None]).astype(jnp.bfloat16), "head").astype(jnp.float32),
    )
    result = (summed / total[..., None]).reshape(row_count, QUERY_HEADS * HEAD_SIZE)
    return result.astype(jnp.bfloat16)


def solution(mesh):
    placed = (
        P(("groups", "req"), None),
        P(("groups", "req"), "head", None),
        P("head", ("groups", "req"), None, None),
        P("head", ("groups", "req"), None),
        P("head", ("groups", "req")),
        P("groups"),
    )
    return jax.shard_map(
        body, mesh=mesh, in_specs=placed, out_specs=P(("groups", "req"), None), check_vma=False
    )
```

profile of v0, /device:TPU:0, one launch (start us, length us, event | category | flops | bytes accessed | tf_op | source)
XLA Modules:
  0.0 151.9 jit_solution(5859482562781935012)
XLA Ops:
  6.5 0.0 copy-start
  6.5 0.0 all-reduce.4.cloned.1.call-start
  6.5 12.4 %copy.56 = bf16[1,2048,2048]{1,2,0:T(8,128)(2,1)} copy(bf16[1,2048,2048]{2,1,0:T(8,128)(2,1)} %param.7) | data formatting | bytes 16777216 | tf_op args[1]
  18.9 0.0 copy-start.1
  18.9 6.1 %fusion.30 = (bf16[2048,1024]{0,1:T(8,128)(2,1)}, bf16[2048,1024]{0,1:T(8,128)(2,1)}) fusion(bf16[2048,2048]{0,1:T(8,128)(2,1)} %bitcast.92), kind=kLoop, calls=%fused_computation.46 | loop fusion | bytes 16777216 | tf_op jit(solution)/shard_map/while/body/eval_jaxpr/slice | solution.py:29
  25.0 0.0 copy-done.1
  25.0 32.5 %all-gather = bf16[8,1,8192]{2,1,0:T(2,128)(2,1)S(1)} all-gather(bf16[1,1,8192]{2,1,0:T(2,128)(2,1)S(1)} %bitcast.98), channel_id=1, replica_groups=mesh['groups'=2,'req'=8,'head'=2] {'req'}, dimensions={0}, use_global_device_ids=true | all-gather | bytes 147456 | tf_op jit(solution)/shard_map/all_gather | solution.py:88
  58.2 0.8 reduce.5
  59.0 3.1 %bitcast_reduce_fusion = (f32[8,8,8]{2,0,1:T(8,128)S(1)}, f32[8,2048,8,8]{1,3,2,0:T(8,128)S(1)}) fusion(bf16[2048,8,128,1]{0,2,3,1:T(8,128)(2,1)} %bitcast.95, bf16[1,8,64,128]{3,1,2,0:T(8,128)(2,1)S(1)} %bitcast.99), kind=kOutput, calls=%fused_computation.2 | convolution fusion | flops 270532096 | bytes 8521728 | tf_op jit(solution)/shard_map/while/body/eval_jaxpr/rkgd,tkd->rkgt/dot_general | solution.py:45
  62.1 0.9 convert_reduce_fusion
  63.0 0.0 copy-start.2
  63.0 4.5 %fusion.7 = f32[8,8,8,128]{3,2,1,0:T(8,128)} fusion(bf16[2048,8,128,1]{0,2,1,3:T(8,128)(2,1)} %bitcast.93, bf16[8,8,8,2048]{3,2,0,1:T(8,128)(2,1)S(1)} %get-tuple-element.30, pred[]{:T(512)S(6)} %eq.2), kind=kOutput, calls=%fused_computation.9 | convolution fusion | flops 268500992 | bytes 6553601 | tf_op jit(solution)/shard_map/while/body/eval_jaxpr/rkgt,tkd->rkgd/dot_general | solution.py:51
  67.4 0.0 all-reduce.4.cloned.1.call-update
  67.5 0.1 reduce.4
  67.6 0.0 copy-done.2
  67.6 0.0 copy-done
  67.6 0.6 gather_fusion
  68.3 0.1 fusion.31
  68.3 0.2 copy.52
  69.2 37.7 %all-reduce = (f32[8,8,8]{2,1,0:T(8,128)S(1)}, f32[8,8,8]{2,1,0:T(8,128)S(1)}) all-reduce(f32[8,8,8]{2,1,0:T(8,128)S(1)} %copy_select_fusion.1, f32[8,8,8]{2,1,0:T(8,128)S(1)} %copy_select_fusion), channel_id=1, replica_groups=mesh['groups'=2,'req'=8,'head'=2] {'req'}, use_global_device_ids=true, to_apply=%region_2.3 | all-reduce | flops 1024 | bytes 8192 | tf_op jit(solution)/shard_map/psum | solution.py:15
  106.9 0.3 fusion.32
  107.1 0.2 convert_reduce_fusion.1
  107.3 0.2 copy.54
  107.5 2.5 %pmax.7 = f32[1,8,8]{2,1,0:T(8,128)S(1)} all-reduce(f32[1,8,8]{2,1,0:T(8,128)S(1)} %get-tuple-element.28), channel_id=1, replica_groups=mesh['groups'=2,'req'=8,'head'=2] {'head'}, use_global_device_ids=true, to_apply=%region_4.5 | all-reduce | flops 64 | bytes 512 | tf_op jit(solution)/shard_map/pmax | solution.py:114
  110.0 29.9 %all-reduce.4.cloned.1.call-done = f32[8,8,8,128]{3,2,1,0:T(8,128)} async-done(((f32[8,8,8,128]{3,2,1,0:T(8,128)}), f32[8,8,8,128]{3,2,1,0:T(8,128)}) %all-reduce.4.cloned.1.call-update) | async-done | bytes 262160 | tf_op jit(solution)/shard_map/psum | solution.py:15
  139.9 1.0 fusion.15
  140.9 3.4 %all-reduce.1 = (bf16[1,8,8,128]{3,2,1,0:T(8,128)(2,1)S(1)}, bf16[8,8]{1,0:T(8,128)(2,1)S(1)}) all-reduce(bf16[1,8,8,128]{3,2,1,0:T(8,128)(2,1)S(1)} %fusion.15, bf16[8,8]{1,0:T(8,128)(2,1)S(1)} %get-tuple-element.35), channel_id=1, replica_groups=mesh['groups'=2,'req'=8,'head'=2] {'head'}, use_global_device_ids=true, to_apply=%region_5.6 | all-reduce | flops 8256 | bytes 33024 | tf_op jit(solution)/shard_map/psum | solution.py:118
  144.4 0.1 fusion.18
  144.4 0.6 copy.90
  (8 shorter events, 0.1 us)
Async XLA Ops:
  6.5 61.1 %copy-start = (bf16[1,16,16,2048]{3,2,1,0:T(8,128)(2,1)S(1)}, bf16[1,16,16,2048]{3,2,1,0:T(8,128)(2,1)}, u32[]{:S(2)}) copy-start(bf16[1,16,16,2048]{3,2,1,0:T(8,128)(2,1)} %param.8) | copy-start | bytes 3145732
  6.5 133.4 %all-reduce.4.cloned.1.call-start = ((), (), s32[]{:S(2)}) async-start(), calls=%async_computation | async-start | bytes 524288 | tf_op jit(solution)/shard_map/psum | solution.py:15
  18.9 6.1 %copy-start.1 = (bf16[1,8192]{1,0:T(2,128)(2,1)S(1)}, bf16[1,8192]{1,0:T(2,128)(2,1)}, u32[]{:S(2)}) copy-start(bf16[1,8192]{1,0:T(2,128)(2,1)} %param.6) | copy-start | bytes 49156
  63.0 4.6 %copy-start.2 = (s32[1,1,16]{2,1,0:T(1,128)S(1)}, s32[1,1,16]{2,1,0:T(1,128)}, u32[]{:S(2)}) copy-start(s32[1,1,16]{2,1,0:T(1,128)} %param.9) | copy-start | bytes 196
Sparse Core Ops, SparseCore 0:
  67.6 72.2 all-reduce.3
where the time goes:
time: 153 us; the launch traced here: 152 us
  blocking collectives  76.1 us (50%)
  waiting for transfers between devices  29.9 us (20%)
  local copies, waits for them, and re-layouts  20.2 us (13%)
  between operations  14.8 us (10%)
  matrix products  8.84 us (6%)
  other arithmetic  2.1 us (1%)
    psum x1, blocking collectives, spread(): return lax.psum(block, axis)  37.7 us
    all_gather x1, blocking collectives, body(): every_query = lax.all_gather(queries, 'req', axis=0, tiled=True)  32.5 us
    psum x1, waiting for transfers between devices, spread(): return lax.psum(block, axis)  29.9 us
    unnamed x8, local copies, waits for them, and re-layouts  13.1 us
    slice x1, local copies, waits for them, and re-layouts, prefix_parts(): block_piece[:, :width_total]  6.05 us
    dot_general x1, matrix products, prefix_state(): jnp.einsum('rkgt,tkd->rkgd', weights, value_rows, preferred_element_type=...  4.45 us
    psum x1, blocking collectives, body(): lax.psum((state[2] * factor[..., None]).astype(jnp.bfloat16), 'head')  3.41 us
    dot_general x1, matrix products, prefix_state(): jnp.einsum('rkgd,tkd->rkgt', page_lookup, key_rows, preferred_element_typ...  3.1 us
  transfers between devices with their start and end apart: 1, of which 1 were waited for; matrix products, arithmetic and copies ran while one was open for 1% of the time, Pallas kernels for 0%

commit v1 on v0

v1 whole, which is shorter than its diff:
```python
import functools
import math

import jax
import jax.numpy as jnp
from jax import lax
from jax.experimental import pallas as pl
from jax.experimental.pallas import tpu as pltpu
from jax.sharding import PartitionSpec as P

QUERY_HEADS = 64
KEY_VALUE_HEADS = 8
HEAD_SIZE = 128
GROUP = QUERY_HEADS // KEY_VALUE_HEADS
PAIRS = KEY_VALUE_HEADS // 2
WIDTH = KEY_VALUE_HEADS * HEAD_SIZE
DUO = 2 * HEAD_SIZE
ROWS = 2 * GROUP
RATE = HEAD_SIZE ** (-0.5) / math.log(2.0)
MESH = pl.DeviceIdType.MESH


def each(first, last, step):
    if last - first <= 8:
        for index in range(first, last):
            step(index)
    else:
        lax.fori_loop(first, last, lambda index, carry: (step(index), carry)[1], 0)


def second_head(shape):
    return lax.rem(lax.broadcasted_iota(jnp.int32, shape, 0), ROWS) >= GROUP


def block_diagonal(block):
    odd = second_head(block.shape)
    zero = jnp.zeros_like(block)
    return jnp.concatenate([jnp.where(odd, zero, block), jnp.where(odd, block, zero)], axis=1)


def contract_last(left, right):
    return lax.dot_general(left, right, (((1,), (1,)), ((), ())), preferred_element_type=jnp.float32)


def own_columns(product):
    left = product[:, :HEAD_SIZE]
    return jnp.where(second_head(left.shape), product[:, HEAD_SIZE:], left)


def kernel(
    n, batch, queries, prefix, pool, table, lengths, owner, out,
    q_in, q_rows, q_own, q_all, keys, values, pages, table_s, length_s, owner_s,
    part_out, stat_out, part_in, stat_in, suffix, suffix_stat, halves, result,
    load_sem, page_sem, key_sem, value_sem, q_send, q_recv, p_send, p_recv, s_send, s_recv, h_send, h_recv,
):
    group = lax.axis_index("groups")
    me = lax.axis_index("req")
    half = lax.axis_index("head")

    q_load = pltpu.make_async_copy(queries, q_in, load_sem.at[0])
    q_load.start()
    small = [
        pltpu.make_async_copy(table, table_s, load_sem.at[1]),
        pltpu.make_async_copy(lengths, length_s, load_sem.at[2]),
        pltpu.make_async_copy(owner, owner_s, load_sem.at[3]),
    ]
    for copy in small:
        copy.start()
    barrier = pltpu.get_barrier_semaphore()

    def greet(step):
        peer = lax.rem(me + step, n)
        pl.semaphore_signal(barrier, inc=1, device_id=(group, peer, half), device_id_type=MESH)

    each(1, n, greet)
    pl.semaphore_signal(barrier, inc=1, device_id=(group, me, 1 - half), device_id_type=MESH)
    page_load = pltpu.make_async_copy(pool.at[0], pages, page_sem)
    page_load.start()
    loads = []
    for pair in range(PAIRS):
        key_load = pltpu.make_async_copy(prefix.at[0, :, pl.ds(pair * DUO, DUO)], keys.at[pair], key_sem.at[pair])
        value_load = pltpu.make_async_copy(
            prefix.at[0, :, pl.ds(WIDTH + pair * DUO, DUO)], values.at[pair], value_sem.at[pair]
        )
        key_load.start()
        value_load.start()
        loads.append((key_load, value_load))

    q_load.wait()
    flat = q_in[...].astype(jnp.float32)
    for head in range(QUERY_HEADS):
        q_rows[pl.ds(head, 1), :] = flat[:, head * HEAD_SIZE : (head + 1) * HEAD_SIZE]
    for pair in range(PAIRS):
        rows = q_rows[pl.ds(pair * ROWS, ROWS), :].astype(jnp.bfloat16)
        q_own[pair] = rows
        q_all[pair, me] = rows

    pl.semaphore_wait(barrier, n)

    def q_copy(pair, step):
        return pltpu.make_async_remote_copy(
            src_ref=q_own.at[pair], dst_ref=q_all.at[pair, me],
            send_sem=q_send.at[pair, step], recv_sem=q_recv.at[pair, step],
            device_id=(group, lax.rem(me + step, n), half), device_id_type=MESH,
        )

    def p_copy(pair, step):
        peer = lax.rem(me + step, n)
        return pltpu.make_async_remote_copy(
            src_ref=part_out.at[pair, peer], dst_ref=part_in.at[me, pair],
            send_sem=p_send.at[pair, step], recv_sem=p_recv.at[pair, step],
            device_id=(group, peer, half), device_id_type=MESH,
        )

    def s_copy(step):
        peer = lax.rem(me + step, n)
        return pltpu.make_async_remote_copy(
            src_ref=stat_out.at[peer], dst_ref=stat_in.at[me],
            send_sem=s_send.at[step], recv_sem=s_recv.at[step],
            device_id=(group, peer, half), device_id_type=MESH,
        )

    for pair in range(PAIRS):
        each(1, n, lambda step, pair=pair: q_copy(pair, step).start())

    for copy in small:
        copy.wait()
    page_count, page_rows = pages.shape[0], pages.shape[1]
    slots = page_count * page_rows
    spot = lax.broadcasted_iota(jnp.int32, (ROWS, slots), 1)
    page, inside = spot // page_rows, lax.rem(spot, page_rows)
    uses = jnp.zeros((ROWS, slots), jnp.float32)
    for slot in range(table_s.shape[2]):
        hit = (page == table_s[0, 0, slot]) & (inside + slot * page_rows < length_s[0, 0])
        uses += jnp.where(hit, 1.0, 0.0)
    page_load.wait()
    for pair in range(PAIRS):
        page_keys = pages[:, :, pair * DUO : (pair + 1) * DUO].reshape(slots, DUO)
        page_values = pages[:, :, WIDTH + pair * DUO : WIDTH + (pair + 1) * DUO].reshape(slots, DUO)
        scores = contract_last(block_diagonal(q_own[pair]), page_keys)
        scores = jnp.where(uses > 0.0, scores, -jnp.inf)
        top = jnp.max(scores, axis=1, keepdims=True)
        weights = jnp.exp2((scores - top) * RATE).astype(jnp.bfloat16).astype(jnp.float32) * uses
        total = jnp.sum(weights, axis=1, keepdims=True)
        summed = jnp.dot(weights.astype(jnp.bfloat16), page_values, preferred_element_type=jnp.float32)
        suffix[pair] = own_columns(summed)
        suffix_stat[pair, 0] = jnp.broadcast_to(top, (ROWS, HEAD_SIZE))
        suffix_stat[pair, 1] = jnp.broadcast_to(total, (ROWS, HEAD_SIZE))

    lane = lax.broadcasted_iota(jnp.int32, (batch, GROUP, HEAD_SIZE), 2)
    for pair in range(PAIRS):
        each(1, n, lambda step, pair=pair: q_copy(pair, step).wait_recv())
        loads[pair][0].wait()
        loads[pair][1].wait()

        def attend(index, pair=pair):
            block = pl.ds(index * batch, batch)
            rows = q_all[pair, block].reshape(batch * ROWS, HEAD_SIZE)
            scores = contract_last(block_diagonal(rows), keys[pair])
            top = jnp.max(scores, axis=1, keepdims=True)
            weights = jnp.exp2((scores - top) * RATE).astype(jnp.bfloat16)
            total = jnp.sum(weights.astype(jnp.float32), axis=1, keepdims=True)
            summed = jnp.dot(weights, values[pair], preferred_element_type=jnp.float32)
            part_out[pair, block] = own_columns(summed).reshape(batch, ROWS, HEAD_SIZE).astype(jnp.bfloat16)
            wide = (batch, 2, GROUP, HEAD_SIZE)
            tops = jnp.broadcast_to(top, (batch * ROWS, HEAD_SIZE)).reshape(wide)
            totals = jnp.broadcast_to(total, (batch * ROWS, HEAD_SIZE)).reshape(wide)
            stats = jnp.zeros((batch, GROUP, HEAD_SIZE), jnp.float32) if pair == 0 else stat_out[block]
            for side in range(2):
                place = 2 * (2 * pair + side)
                stats = jnp.where(lane == place, tops[:, side], stats)
                stats = jnp.where(lane == place + 1, totals[:, side], stats)
            stat_out[block] = stats

        each(0, n // batch, attend)
        each(1, n, lambda step, pair=pair: p_copy(pair, step).start())
    each(1, n, lambda step: s_copy(step).start())
    for pair in range(PAIRS):
        part_in[me, pair] = part_out[pair, me]
    stat_in[me] = stat_out[me]

    for pair in range(PAIRS):
        each(1, n, lambda step, pair=pair: p_copy(pair, step).wait_recv())
    each(1, n, lambda step: s_copy(step).wait_recv())

    root = owner_s[0]
    arrived = part_in[root]
    stats = stat_in[root]
    mine = jnp.zeros((GROUP, HEAD_SIZE), jnp.float32)
    narrow = lax.broadcasted_iota(jnp.int32, (GROUP, HEAD_SIZE), 1)
    for head in range(KEY_VALUE_HEADS):
        pair, side = head // 2, pl.ds((head % 2) * GROUP, GROUP)
        top_a = jnp.broadcast_to(stats[:, 2 * head : 2 * head + 1], (GROUP, HEAD_SIZE))
        total_a = jnp.broadcast_to(stats[:, 2 * head + 1 : 2 * head + 2], (GROUP, HEAD_SIZE))
        low = (head % 2) * GROUP
        sum_a = arrived[pair].astype(jnp.float32)[low : low + GROUP]
        top_b, total_b, sum_b = suffix_stat[pair, 0, side], suffix_stat[pair, 1, side], suffix[pair, side]
        top = jnp.maximum(top_a, top_b)
        early, later = jnp.exp2((top_a - top) * RATE), jnp.exp2((top_b - top) * RATE)
        halves[half, head] = sum_a * early + sum_b * later
        mine = jnp.where(narrow == 2 * head, top, mine)
        mine = jnp.where(narrow == 2 * head + 1, total_a * early + total_b * later, mine)
    halves[half, KEY_VALUE_HEADS] = mine
    swap = pltpu.make_async_remote_copy(
        src_ref=halves.at[half], dst_ref=halves.at[half], send_sem=h_send, recv_sem=h_recv,
        device_id=(group, me, 1 - half), device_id_type=MESH,
    )
    swap.start()
    swap.wait_recv()
    stat_a, stat_b = halves[0, KEY_VALUE_HEADS], halves[1, KEY_VALUE_HEADS]
    for head in range(KEY_VALUE_HEADS):
        full = (GROUP, HEAD_SIZE)
        top_a = jnp.broadcast_to(stat_a[:, 2 * head : 2 * head + 1], full)
        top_b = jnp.broadcast_to(stat_b[:, 2 * head : 2 * head + 1], full)
        total_a = jnp.broadcast_to(stat_a[:, 2 * head + 1 : 2 * head + 2], full)
        total_b = jnp.broadcast_to(stat_b[:, 2 * head + 1 : 2 * head + 2], full)
        top = jnp.maximum(top_a, top_b)
        early, later = jnp.exp2((top_a - top) * RATE), jnp.exp2((top_b - top) * RATE)
        summed = halves[0, head] * early + halves[1, head] * later
        result[pl.ds(head * GROUP, GROUP), :] = summed / (total_a * early + total_b * later)
    for head in range(QUERY_HEADS):
        out[:, head * HEAD_SIZE : (head + 1) * HEAD_SIZE] = result[pl.ds(head, 1), :].astype(out.dtype)

    for pair in range(PAIRS):
        each(1, n, lambda step, pair=pair: q_copy(pair, step).wait_send())
        each(1, n, lambda step, pair=pair: p_copy(pair, step).wait_send())
    each(1, n, lambda step: s_copy(step).wait_send())
    swap.wait_send()


def body(n, queries, prefix_cache, paged_pool_cache, block_table, lengths, owner):
    length = prefix_cache.shape[1]
    batch = math.gcd(n, 8)
    anywhere = pl.BlockSpec(memory_space=pl.ANY)
    bf16, f32 = jnp.bfloat16, jnp.float32
    dma = pltpu.SemaphoreType.DMA
    return pl.pallas_call(
        functools.partial(kernel, n, batch),
        out_shape=jax.ShapeDtypeStruct(queries.shape, bf16),
        in_specs=[anywhere] * 6,
        out_specs=pl.BlockSpec(memory_space=pltpu.VMEM),
        scratch_shapes=[
            pltpu.VMEM(queries.shape, bf16),
            pltpu.VMEM((QUERY_HEADS, HEAD_SIZE), f32),
            pltpu.VMEM((PAIRS, ROWS, HEAD_SIZE), bf16),
            pltpu.VMEM((PAIRS, n, ROWS, HEAD_SIZE), bf16),
            pltpu.VMEM((PAIRS, length, DUO), bf16),
            pltpu.VMEM((PAIRS, length, DUO), bf16),
            pltpu.VMEM(paged_pool_cache.shape[1:], bf16),
            pltpu.SMEM(block_table.shape, jnp.int32),
            pltpu.SMEM(lengths.shape, jnp.int32),
            pltpu.SMEM(owner.shape, jnp.int32),
            pltpu.VMEM((PAIRS, n, ROWS, HEAD_SIZE), bf16),
            pltpu.VMEM((n, GROUP, HEAD_SIZE), f32),
            pltpu.VMEM((n, PAIRS, ROWS, HEAD_SIZE), bf16),
            pltpu.VMEM((n, GROUP, HEAD_SIZE), f32),
            pltpu.VMEM((PAIRS, ROWS, HEAD_SIZE), f32),
            pltpu.VMEM((PAIRS, 2, ROWS, HEAD_SIZE), f32),
            pltpu.VMEM((2, KEY_VALUE_HEADS + 1, GROUP, HEAD_SIZE), f32),
            pltpu.VMEM((QUERY_HEADS, HEAD_SIZE), f32),
            dma((4,)),
            dma,
            dma((PAIRS,)),
            dma((PAIRS,)),
            dma((PAIRS, n)),
            dma((PAIRS, n)),
            dma((PAIRS, n)),
            dma((PAIRS, n)),
            dma((n,)),
            dma((n,)),
            dma,
            dma,
        ],
        compiler_params=pltpu.CompilerParams(collective_id=0, has_side_effects=True),
    )(queries, prefix_cache, paged_pool_cache, block_table, lengths, owner)


def solution(mesh):
    placed = (
        P(("groups", "req"), None),
        P(("groups", "req"), "head", None),
        P("head", ("groups", "req"), None, None),
        P("head", ("groups", "req"), None),
        P("head", ("groups", "req")),
        P("groups"),
    )
    return jax.shard_map(
        functools.partial(body, mesh.shape["req"]),
        mesh=mesh, in_specs=placed, out_specs=P(("groups", "req"), None), check_vma=False,
    )
```

time: 153 us -> 25 us (0.16)
  blocking collectives: 76.1 us -> 0 us
  waiting for transfers between devices: 29.9 us -> 0 us
  Pallas kernels: 0 us -> 22 us
  local copies, waits for them, and re-layouts: 20.2 us -> 1.41 us
  between operations: 14.8 us -> 1.3 us
  matrix products: 8.84 us -> 0 us
  other arithmetic: 2.1 us -> 0 us
    psum x2 -> x0, blocking collectives: 41.1 us -> none  [the longest x1 37.7 us: spread(): return lax.psum(block, axis)]
    all_gather x1 -> x0, blocking collectives: 32.5 us -> none  [body(): every_query = lax.all_gather(queries, 'req', axis=0, tiled=True)]
    psum x1 -> x0, waiting for transfers between devices: 29.9 us -> none  [spread(): return lax.psum(block, axis)]
    pallas_call x0 -> x1, Pallas kernels: none -> 22 us  [body(): pl.pallas_call(functools.partial(kernel, n, batch), out_shape=jax.ShapeDt...]
    unnamed x8 -> x1, local copies, waits for them, and re-layouts: 13.1 us -> 1.41 us
    dot_general x4 -> x0, matrix products: 8.84 us -> none  [the longest x1 4.45 us: prefix_state(): jnp.einsum('rkgt,tkd->rkgd', weights, value_rows, preferred_element_type=...]
    slice x4 -> x0, local copies, waits for them, and re-layouts: 6.54 us -> none  [the longest x1 6.05 us: prefix_parts(): block_piece[:, :width_total]]
    pmax x1 -> x0, blocking collectives: 2.47 us -> none  [body(): highest = lax.pmax(state[0], 'head')]
  transfers between devices with their start and end apart: 1 -> 0, of which waited for: 1 -> 0; matrix products, arithmetic and copies ran while one was open for 1% -> 0% of each run, Pallas kernels for 0% -> 0%
where the time goes in v1:
time: 25 us; the launch traced here: 24.7 us
  Pallas kernels  22 us (88%)
  local copies, waits for them, and re-layouts  1.41 us (6%)
  between operations  1.3 us (5%)
    pallas_call x1, Pallas kernels, body(): pl.pallas_call(functools.partial(kernel, n, batch), out_shape=jax.ShapeDt...  22 us
    unnamed x1, local copies, waits for them, and re-layouts  1.41 us

profile of v1, /device:TPU:0, one launch (start us, length us, event | category | flops | bytes accessed | tf_op | source)
XLA Modules:
  0.0 24.7 jit_solution(9073374293462354269)
XLA Ops:
  1.3 22.0 %shard_map.64 = bf16[1,8192]{1,0:T(2,128)(2,1)} custom-call(bf16[1,8192]{1,0:T(2,128)(2,1)} %queries.1, bf16[1,2048,2048]{2,1,0:T(8,128)(2,1)} %prefix.1, bf16[1,16,16,2048]{3,2,1,0:T(8,128)(2,1)} %pool.1, s32[1,1,16]{2,1,0:T(1,128)} %table.1, s32[1,1]{1,0:T(1,128)S(6)} %copy.8.lengths, s32[1]{0:T(128)S(6)} %copy.9.owner), custom_call_target="tpu_custom_call" | custom-call | tf_op jit(solution)/shard_map/pallas_call | solution.py:237
  23.3 1.4 %copy.10 = bf16[1,8192]{1,0:T(2,128)(2,1)} copy(bf16[1,8192]{1,0:T(2,128)(2,1)} %shard_map.64) | data formatting | bytes 32768
